TPU v7x, 32 devices: a whole 2x2x4 slice. The times are simulated.
32 devices in a mesh: ha: 8 (over z, core), wa: 2 (over y), ba: 2 (over x).
Axes of the slice: x: 2, y: 2, z: 4, core: 2. Of those that a mesh axis runs over, the one named last changes fastest.
Arguments:
- tokens: bfloat16 [2, 128, 64, 384], P('ba', 'ha', 'wa'), may hold values from -6 to 6
- cotangent: bfloat16 [2, 128, 64, 384], P('ba', 'ha', 'wa'), may hold values from -6 to 6
- w_qkv: bfloat16 [384, 1152], replicated, may hold values from -0.20412415 to 0.20412415
- w_proj: bfloat16 [384, 384], replicated, may hold values from -0.3125 to 0.3125
- table_logits: float32 [12, 225], replicated, may hold values from -6 to 6
- logit_scale: float32 [12], replicated, may hold values from 1 to 5.5
- gain: float32 [384], replicated, may hold values from 0.5 to 1.5
Outputs:
- d_tokens: bfloat16 [2, 128, 64, 384], P('ba', 'ha', 'wa')
- d_wqkv: float32 [384, 1152], P(None, 'ba')
- d_wproj: float32 [384, 384], P(None, 'ba')
- d_table: float32 [12, 225], replicated
- d_scale: float32 [12], replicated
- d_gain: float32 [384], replicated
All inputs are finite; a program needn't handle non-finite values.
Results may differ from a plain program's by a relative error of at most 0.01.
The roundings to bfloat16 on the way count: a program that leaves them out, or rounds other values in their place, can miss the bound.
Values may be sent and summed in bfloat16 or wider, within the bound.
A program may use at most 64 MiB of HBM per device.

v0:
```python
import math
import jax
import jax.numpy as jnp
from jax import lax
from jax.sharding import PartitionSpec as P

WIN = 8
EPS_NORM = 1e-05
MASK_FILL = -100.0
SCALE_CAP = math.log(100.0)
BIAS_RANGE = 16.0
HIGHEST = lax.Precision.HIGHEST


def from_behind(block, axis, distance):
    devices = range(lax.axis_size(axis))
    route = [((i - distance) % len(devices), i) for i in devices]
    return lax.ppermute(block, axis, route)


def coarse_product(form, left, right):
    return jnp.einsum(form, left, right, preferred_element_type=jnp.float32)


def fine_product(form, left, right):
    return jnp.einsum(form, left, right, precision=HIGHEST)


def to_windows(block, window):
    images, height, width, depth = block.shape
    tiles = block.reshape(images, height // window, window, width // window, window, depth)
    tiles = tiles.transpose(0, 1, 3, 2, 4, 5)
    return tiles.reshape(images, height // window * (width // window), window * window, depth)


def from_windows(tiles, images, height, width, window):
    depth = tiles.shape[-1]
    grid = tiles.reshape(images, height // window, width // window, window, window, depth)
    return grid.transpose(0, 1, 3, 2, 4, 5).reshape(images, height, width, depth)


def position_onehot(window):
    places = jnp.arange(window * window, dtype=jnp.int32)
    row_of = places // window
    col_of = places % window
    offset = (row_of[:, None] - row_of[None, :] + window - 1) * (2 * window - 1) + (
        col_of[:, None] - col_of[None, :] + window - 1
    )
    entries = jnp.arange((2 * window - 1) ** 2, dtype=jnp.int32)
    return (offset.reshape(-1)[:, None] == entries[None, :]).astype(jnp.float32)


def region_of(coords, extent, window):
    return (coords >= extent - window).astype(jnp.int32) + (coords >= extent - window // 2).astype(
        jnp.int32
    )


def region_mask(row_start, col_start, rows, cols, height, width, window):
    row_label = region_of(row_start + jnp.arange(rows, dtype=jnp.int32), height, window)
    col_label = region_of(col_start + jnp.arange(cols, dtype=jnp.int32), width, window)
    labels = row_label[:, None] * 3 + col_label[None, :]
    labels = labels.reshape(rows // window, window, cols // window, window).transpose(0, 2, 1, 3)
    labels = labels.reshape(-1, window * window)
    return jnp.where(labels[:, :, None] != labels[:, None, :], MASK_FILL, 0.0).astype(jnp.float32)


def grads_region(block, grad_block, row_start, col_start, height, width, window, params):
    w_qkv, w_proj, table_logits, logit_scale, gain = params
    images, rows, cols, depth = block.shape
    heads = logit_scale.shape[0]
    head_dim = depth // heads
    tiles = to_windows(block, window)
    grad_tiles = to_windows(grad_block, window)
    count = tiles.shape[1]
    length = window * window
    flat = tiles.reshape(-1, depth)
    qkv = jnp.dot(flat, w_qkv, preferred_element_type=jnp.float32).astype(jnp.bfloat16)
    qkv = qkv.reshape(images, count, length, 3, heads, head_dim)
    query = qkv[:, :, :, 0].astype(jnp.float32)
    keys = qkv[:, :, :, 1].astype(jnp.float32)
    values = qkv[:, :, :, 2]
    query_inv = lax.rsqrt(jnp.sum(query * query, -1, keepdims=True) + 1.0)
    key_inv = lax.rsqrt(jnp.sum(keys * keys, -1, keepdims=True) + 1.0)
    unit_query = query * query_inv
    unit_key = keys * key_inv
    scale = jnp.exp(jnp.minimum(logit_scale, SCALE_CAP))
    onehot = position_onehot(window)
    sigma = jax.nn.sigmoid(table_logits)
    rel_bias = jnp.dot(sigma * BIAS_RANGE, onehot.T, precision=HIGHEST).reshape(
        heads, length, length
    )
    mask = region_mask(row_start, col_start, rows, cols, height, width, window)
    cosine = fine_product("bnqhd,bnkhd->bnhqk", unit_query, unit_key)
    scores = scale[:, None, None] * cosine + rel_bias[None, None] + mask[None, :, None]
    top = jnp.max(scores, -1, keepdims=True)
    expo = jnp.exp(scores - top)
    probs = expo / jnp.sum(expo, -1, keepdims=True)
    probs_low = probs.astype(jnp.bfloat16)
    attended = (
        coarse_product("bnhqk,bnkhd->bnqhd", probs_low, values)
        .astype(jnp.bfloat16)
        .reshape(-1, depth)
    )
    proj = jnp.dot(attended, w_proj, preferred_element_type=jnp.float32)
    centre = proj - jnp.mean(proj, -1, keepdims=True)
    inv_std = lax.rsqrt(jnp.mean(centre * centre, -1, keepdims=True) + EPS_NORM)
    normed = centre * inv_std
    upstream = grad_tiles.reshape(-1, depth).astype(jnp.float32)
    d_gain = jnp.sum(upstream * normed, 0)
    scaled = upstream * gain
    d_proj = inv_std * (
        scaled
        - jnp.mean(scaled, -1, keepdims=True)
        - normed * jnp.mean(scaled * normed, -1, keepdims=True)
    )
    d_proj = d_proj.astype(jnp.bfloat16)
    d_wproj = jnp.dot(attended.T, d_proj, preferred_element_type=jnp.float32)
    d_att = jnp.dot(d_proj, w_proj.T, preferred_element_type=jnp.float32).astype(jnp.bfloat16)
    d_att = d_att.reshape(images, count, length, heads, head_dim)
    d_probs = coarse_product("bnqhd,bnkhd->bnhqk", d_att, values)
    d_values = coarse_product("bnhqk,bnqhd->bnkhd", probs_low, d_att)
    d_scores = probs * (d_probs - jnp.sum(d_probs * probs, -1, keepdims=True))
    d_bias = jnp.sum(d_scores, (0, 1)).reshape(heads, length * length)
    d_table = jnp.dot(d_bias, onehot, precision=HIGHEST) * (BIAS_RANGE * sigma * (1.0 - sigma))
    live = (logit_scale < SCALE_CAP).astype(jnp.float32)
    d_scale = jnp.sum(d_scores * cosine, (0, 1, 3, 4)) * scale * live
    d_cos = d_scores * scale[:, None, None]
    d_unit_q = fine_product("bnhqk,bnkhd->bnqhd", d_cos, unit_key)
    d_unit_k = fine_product("bnhqk,bnqhd->bnkhd", d_cos, unit_query)
    d_query = query_inv * (
        d_unit_q - unit_query * jnp.sum(unit_query * d_unit_q, -1, keepdims=True)
    )
    d_key = key_inv * (d_unit_k - unit_key * jnp.sum(unit_key * d_unit_k, -1, keepdims=True))
    d_qkv = jnp.stack([d_query, d_key, d_values], 3).astype(jnp.bfloat16).reshape(-1, 3 * depth)
    d_wqkv = jnp.dot(flat.T, d_qkv, preferred_element_type=jnp.float32)
    d_flat = jnp.dot(d_qkv, w_qkv.T, preferred_element_type=jnp.float32).astype(jnp.bfloat16)
    d_block = from_windows(d_flat.reshape(images, count, length, depth), images, rows, cols, window)
    return (d_block, (d_wqkv, d_wproj, d_table, d_scale, d_gain))


def shift_in(tokens, cotangent, shift):
    stacked = jnp.stack([tokens, cotangent])
    below = from_behind(stacked[:, :, :shift], "ha", -1)
    tall = jnp.concatenate([stacked[:, :, shift:], below], 2)
    beside = from_behind(tall[:, :, :, :shift], "wa", -1)
    moved = jnp.concatenate([tall[:, :, :, shift:], beside], 3)
    return (moved[0], moved[1])


def shift_out(grads, shift):
    rows = grads.shape[1]
    cols = grads.shape[2]
    right = from_behind(grads[:, :, cols - shift :], "wa", 1)
    wide = jnp.concatenate([right, grads[:, :, : cols - shift]], 2)
    lower = from_behind(wide[:, rows - shift :], "ha", 1)
    return jnp.concatenate([lower, wide[:, : rows - shift]], 1)


def shards(tokens, cotangent, w_qkv, w_proj, table_logits, logit_scale, gain):
    rows = tokens.shape[1]
    cols = tokens.shape[2]
    shift = WIN // 2
    height = rows * lax.axis_size("ha")
    width = cols * lax.axis_size("wa")
    row_base = lax.axis_index("ha") * rows
    col_base = lax.axis_index("wa") * cols
    params = (w_qkv, w_proj, table_logits, logit_scale, gain)
    moved, moved_grad = shift_in(tokens, cotangent, shift)
    d_moved, parts = grads_region(moved, moved_grad, row_base, col_base, height, width, WIN, params)
    back = shift_out(d_moved, shift)
    d_tokens = (cotangent.astype(jnp.float32) + back.astype(jnp.float32)).astype(jnp.bfloat16)
    d_wqkv, d_wproj, d_table, d_scale, d_gain = parts
    half_qkv, half_proj = (
        lax.psum_scatter(d_wqkv.astype(jnp.bfloat16), "ba", scatter_dimension=1, tiled=True).astype(
            jnp.float32
        ),
        lax.psum_scatter(
            d_wproj.astype(jnp.bfloat16), "ba", scatter_dimension=1, tiled=True
        ).astype(jnp.float32),
    )
    half_qkv, half_proj = lax.psum((half_qkv, half_proj), ("ha", "wa"))
    d_table, d_scale, d_gain = lax.psum((d_table, d_scale, d_gain), ("ha", "wa", "ba"))
    return (d_tokens, half_qkv, half_proj, d_table, d_scale, d_gain)


def solution(mesh):
    return jax.shard_map(
        shards,
        mesh=mesh,
        in_specs=(P("ba", "ha", "wa", None), P("ba", "ha", "wa", None), P(), P(), P(), P(), P()),
        out_specs=(P("ba", "ha", "wa", None), P(None, "ba"), P(None, "ba"), P(), P(), P()),
        check_vma=False,
    )
```

profile of v0, /device:TPU:0, one launch (start us, length us, event | category | flops | bytes accessed | tf_op | source)
XLA Modules:
  0.0 213.7 jit_solution(15621993046436900654)
XLA Ops:
  8.3 4.6 %collective-permute-start = (bf16[2,1,4,32,384]{4,3,2,1,0:T(8,128)(2,1)S(1)}, bf16[2,1,4,32,384]{4,3,2,1,0:T(8,128)(2,1)S(1)}, u32[]{:S(2)}, u32[]{:S(2)}) collective-permute-start(bf16[2,1,4,32,384]{4,3,2,1,0:T(8,128)(2,1)S(1)} %pad_maximum_fusion.2), channel_id=1, source_target_pairs={{4,0},{8,4},{12,8},{16,12},{20,16},{24,20},{28,24},{0,28},{5,1},{9... | collective-permute-start | bytes 589832 | tf_op jit(solution)/shard_map/ppermute | solution.py:18
  15.2 2.0 fusion.2
  18.3 1.6 collective-permute-start.1
  20.2 2.8 %collective-permute-done.1 = bf16[2,1,16,4,384]{4,3,2,1,0:T(4,128)(2,1)S(1)} collective-permute-done((bf16[2,1,16,4,384]{4,3,2,1,0:T(4,128)(2,1)S(1)}, bf16[2,1,16,4,384]{4,3,2,1,0:T(4,128)(2,1)S(1)}, u32[]{:S(2)}, u32[]{:S(2)}) %collective-permute-start.1) | collective-permute-done | bytes 98336 | tf_op jit(solution)/shard_map/ppermute | solution.py:18
  26.1 3.0 %reshape.449 = bf16[1,8,64,3,12,32]{2,1,5,4,3,0:T(8,128)(2,1)} reshape(bf16[512,1152]{0,1:T(8,128)(2,1)S(1)} %copy.82) | data formatting | bytes 2359296 | tf_op jit(solution)/shard_map/reshape | solution.py:79
  29.2 1.8 fusion.67
  31.7 5.2 %fusion.29 = f32[8,12,64,64]{2,3,1,0:T(8,128)S(1)} fusion(f32[8,64,12]{1,2,0:T(8,128)S(1)} %add_rsqrt_fusion.1, f32[8,64,12]{1,2,0:T(8,128)S(1)} %add_rsqrt_fusion, bf16[1,8,64,1,12,32]{2,1,5,4,3,0:T(8,128)(2,1)S(1)} %get-tuple-element.16, bf16[1,8,64,1,12,32]{2,1,5,4,3,0:T(8,128)(2,1)S(1)} %get-tuple-element.17), kind=kOutput, calls=%fused_computation.41 | convolution fusion | flops 151781376 | bytes 2408448 | tf_op jit(solution)/shard_map/bnqhd,bnkhd->bnhqk/dot_general | solution.py:26
  42.1 1.6 fusion.69
  44.8 2.3 %copy.90 = f32[512,384]{0,1:T(8,128)} copy(f32[512,384]{1,0:T(8,128)} %bitcast.140) | data formatting | bytes 1572864 | tf_op jit(solution)/shard_map/convert_element_type | solution.py:109
  48.3 1.4 multiply_reduce_fusion.2
  49.8 1.4 multiply_convert_fusion
  53.0 1.3 reshape.452
  54.3 3.6 %multiply_reduce_fusion.1 = (f32[8,12,64]{2,1,0:T(8,128)S(1)}, f32[8,12,64,64]{2,3,1,0:T(8,128)S(1)}) fusion(f32[8,12,64,64]{2,3,1,0:T(8,128)} %copy-done.3, f32[8,12,64]{2,1,0:T(8,128)S(1)} %get-tuple-element.21, bf16[1,8,64,1,12,32]{2,1,5,4,3,0:T(8,128)(2,1)} %copy-done.14, bf16[8,64,12,32]{1,0,3,2:T(8,128)(2,1)} %reshape.452), kind=kOutput, calls=%fused_computation.7 | convolution fusion | flops 26339328 | bytes 3981312 | tf_op jit(solution)/shard_map/bnqhd,bnkhd->bnhqk/dot_general | solution.py:22
  58.6 2.2 %multiply_reduce_fusion = (f32[12]{0:T(128)S(1)}, f32[12,64,64]{1,2,0:T(8,128)}, f32[8,12,64,64]{2,3,1,0:T(8,128)S(1)}) fusion(f32[8,12,64,64]{2,3,1,0:T(8,128)S(1)} %copy-done.2, f32[8,12,64,64]{2,3,1,0:T(8,128)S(1)} %get-tuple-element.26, f32[8,12,64]{2,1,0:T(8,128)S(1)} %get-tuple-element.25, f32[8,12,64,64]{2,3,1,0:T(8,128)S(1)} %copy-done.4, ...), kind=kLoop, calls=%fused_computation.5 | loop fusion | flops 2310132 | bytes 6537264 | tf_op jit(solution)/shard_map/reduce_sum | solution.py:127
  60.7 4.3 %fusion.22 = (f32[8,64,12]{1,2,0:T(8,128)S(1)}, f32[8,12,32,64]{3,2,1,0:T(8,128)}) fusion(f32[8,64,12]{1,2,0:T(8,128)S(1)} %add_rsqrt_fusion.1, bf16[1,8,64,1,12,32]{2,1,5,4,3,0:T(8,128)(2,1)S(1)} %get-tuple-element.17, f32[8,12,64,64]{2,3,1,0:T(8,128)S(1)} %get-tuple-element.15, f32[12]{0:T(128)S(1)} %minimum_exponential_fusion, ...), kind=kOutput, calls=%fused_computation.35 | convolution fusion | flops 152561664 | bytes 3219504 | tf_op jit(solution)/shard_map/bnhqk,bnkhd->bnqhd/dot_general | solution.py:26
  65.0 6.8 %fusion.18 = (f32[8,64,12]{1,2,0:T(8,128)}, f32[8,12,32,64]{3,2,1,0:T(8,128)}) fusion(f32[8,64,12]{1,2,0:T(8,128)S(1)} %add_rsqrt_fusion, bf16[1,8,64,1,12,32]{2,1,5,4,3,0:T(8,128)(2,1)S(1)} %get-tuple-element.16, f32[8,12,64,64]{2,3,1,0:T(8,128)S(1)} %get-tuple-element.15, f32[12]{0:T(128)S(1)} %minimum_exponential_fusion, ...), kind=kOutput, calls=%fused_computation.31 | convolution fusion | flops 152561664 | bytes 3219504 | tf_op jit(solution)/shard_map/bnhqk,bnqhd->bnkhd/dot_general | solution.py:26
  73.1 2.6 %fusion.21 = (bf16[1,8,64,1,12,32]{2,5,4,1,3,0:T(8,128)(2,1)S(1)}, bf16[1,8,64,1,12,32]{2,5,4,1,3,0:T(8,128)(2,1)S(1)}) fusion(f32[8,12,32,64]{3,2,1,0:T(8,128)} %get-tuple-element.28, f32[8,64,12]{1,2,0:T(8,128)} %get-tuple-element.27, f32[8,64,12]{1,2,0:T(8,128)S(1)} %add_rsqrt_fusion, bf16[1,8,64,1,12,32]{2,1,5,4,3,0:T(8,128)(2,1)S(1)} %get-tuple-element.16, ...), kind=kLoop, calls=%fused_computation.34 | loop fusion | flops 2359296 | bytes 3244032 | tf_op jit(solution)/shard_map/stack | solution.py:135
  76.3 2.7 %copy.98 = bf16[1,8,64,3,12,32]{2,1,5,4,3,0:T(8,128)(2,1)S(1)} copy(bf16[1,8,64,3,12,32]{2,5,4,1,3,0:T(8,128)(2,1)S(1)} %maximum_convert_fusion) | data formatting | bytes 2359296 | tf_op jit(solution)/shard_map/convert_element_type | solution.py:135
  79.1 2.4 %convert_element_type.207 = bf16[512,1152]{0,1:T(8,128)(2,1)} reshape(bf16[1,8,64,3,12,32]{2,1,5,4,3,0:T(8,128)(2,1)S(1)} %copy.98) | data formatting | bytes 2359296 | tf_op jit(solution)/shard_map/convert_element_type | solution.py:135
  81.5 3.1 %convolution_convert_fusion.1 = bf16[384,1152]{0,1:T(8,128)(2,1)} fusion(bf16[512,1152]{0,1:T(8,128)(2,1)} %convert_element_type.207, bf16[512,384]{1,0:T(8,128)(2,1)} %bitcast.142), kind=kOutput, calls=%fused_computation.15 | convolution fusion | flops 453427200 | bytes 2457600 | tf_op jit(solution)/shard_map/dot_general | solution.py:136
  86.8 1.6 collective-permute-start.2
  88.4 1.4 fusion.41
  91.1 39.5 %all-reduce = (f32[12,225]{1,0:T(8,128)}, f32[12]{0:T(128)}, f32[384]{0:T(512)}) all-reduce(f32[12,225]{1,0:T(8,128)S(1)} %fusion.41, f32[12]{0:T(128)S(1)} %compare_select_fusion.1, f32[384]{0:T(512)S(1)} %get-tuple-element.8), channel_id=1, replica_groups=mesh['ha'=8,'wa'=2,'ba'=2] {'ha','wa','ba'}, use_global_device_ids=true, to_apply=%region_16.17 | all-reduce | flops 3096 | bytes 24768 | tf_op jit(solution)/shard_map/psum | solution.py:183
  131.5 75.2 %all-reduce.3 = (f32[384,576]{0,1:T(8,128)}, f32[384,192]{0,1:T(8,128)}) all-reduce(bf16[384,576]{0,1:T(8,128)(2,1)} %reduce-scatter.3.cloned.1.call-done, bf16[384,192]{0,1:T(8,128)(2,1)} %reduce-scatter.5.cloned.1.call-done), channel_id=1, replica_groups=mesh['ha'=8,'wa'=2,'ba'=2] {'ha','wa'}, use_global_device_ids=true, to_apply=%region_12.13 | all-reduce | flops 294912 | bytes 1769472 | tf_op jit(solution)/shard_map/psum | solution.py:182
  (99 shorter events, 24.6 us)
Async XLA Ops:
  7.2 17.5 %copy-start = (bf16[384,1152]{1,0:T(8,128)(2,1)S(1)}, bf16[384,1152]{1,0:T(8,128)(2,1)}, u32[]{:S(2)}) copy-start(bf16[384,1152]{1,0:T(8,128)(2,1)} %param.9) | copy-start | bytes 2654212
  7.2 8.0 %copy-start.17 = (f32[12,225]{1,0:T(8,128)S(1)}, f32[12,225]{1,0:T(8,128)}, u32[]{:S(2)}) copy-start(f32[12,225]{1,0:T(8,128)} %param.11) | copy-start | bytes 32404
  7.2 124.3 %reduce-scatter.5.cloned.1.call-start = ((), (), s32[]{:S(2)}) async-start(), calls=%async_computation.3 | async-start | bytes 442368 | tf_op jit(solution)/shard_map/reduce_scatter | solution.py:178
  8.3 10.0 %collective-permute-start = (bf16[2,1,4,32,384]{4,3,2,1,0:T(8,128)(2,1)S(1)}, bf16[2,1,4,32,384]{4,3,2,1,0:T(8,128)(2,1)S(1)}, u32[]{:S(2)}, u32[]{:S(2)}) collective-permute-start(bf16[2,1,4,32,384]{4,3,2,1,0:T(8,128)(2,1)S(1)} %pad_maximum_fusion.2), channel_id=1, source_target_pairs={{4,0},{8,4},{12,8},{16,12},{20,16},{24,20},{28,24},{0,28},{5,1},{9... | collective-permute-start | bytes 589832 | tf_op jit(solution)/shard_map/ppermute | solution.py:18
  14.0 4.3 %copy-start.18 = (f32[12]{0:T(128)S(1)}, f32[12]{0:T(128)}, u32[]{:S(2)}) copy-start(f32[12]{0:T(128)} %param.12) | copy-start | bytes 148
  18.3 4.7 %collective-permute-start.1 = (bf16[2,1,16,4,384]{4,3,2,1,0:T(4,128)(2,1)S(1)}, bf16[2,1,16,4,384]{4,3,2,1,0:T(4,128)(2,1)S(1)}, u32[]{:S(2)}, u32[]{:S(2)}) collective-permute-start(bf16[2,1,16,4,384]{4,3,2,1,0:T(4,128)(2,1)S(1)} %pad_maximum_fusion.4), channel_id=1, source_target_pairs={{2,0},{0,2},{3,1},{1,3},{6,4},{4,6},{7,5},{5,7},{10,8},{8,10},{11,... | collective-permute-start | bytes 294920 | tf_op jit(solution)/shard_map/ppermute | solution.py:18
  30.9 7.7 %copy-start.14 = (bf16[1,8,64,1,12,32]{2,1,5,4,3,0:T(8,128)(2,1)}, bf16[1,8,64,1,12,32]{2,1,5,4,3,0:T(8,128)(2,1)S(1)}, u32[]{:S(2)}) copy-start(bf16[1,8,64,1,12,32]{2,1,5,4,3,0:T(8,128)(2,1)S(1)} %get-tuple-element.18) | copy-start | bytes 1179652
  31.7 5.2 %copy-start.10 = (f32[12,64,64]{1,2,0:T(8,128)S(1)}, f32[12,64,64]{1,2,0:T(8,128)}, u32[]{:S(2)}) copy-start(f32[12,64,64]{1,2,0:T(8,128)} %copy.85) | copy-start | bytes 589828
  31.7 5.2 %copy-start.13 = (f32[8,64,64]{1,2,0:T(8,128)S(1)}, f32[8,64,64]{1,2,0:T(8,128)}, u32[]{:S(2)}) copy-start(f32[8,64,64]{1,2,0:T(8,128)} %compare_select_fusion) | copy-start | bytes 393220
  36.9 1.7 copy-start.1
  38.6 1.7 copy-start.3
  42.1 1.7 copy-start.6
  43.9 3.2 %copy-start.16 = (f32[384]{0:T(512)S(1)}, f32[384]{0:T(512)}, u32[]{:S(2)}) copy-start(f32[384]{0:T(512)} %param.13) | copy-start | bytes 4612
  49.8 1.4 copy-start.12
  49.8 1.9 copy-start.5
  54.3 3.6 %copy-start.2 = (f32[8,12,64,64]{2,3,1,0:T(8,128)S(1)}, f32[8,12,64,64]{2,3,1,0:T(8,128)}, u32[]{:S(2)}) copy-start(f32[8,12,64,64]{2,3,1,0:T(8,128)} %copy-done.1) | copy-start | bytes 4718596
  54.3 4.3 %copy-start.4 = (f32[8,12,64,64]{2,3,1,0:T(8,128)S(1)}, f32[8,12,64,64]{2,3,1,0:T(8,128)}, u32[]{:S(2)}) copy-start(f32[8,12,64,64]{2,3,1,0:T(8,128)} %copy-done.3) | copy-start | bytes 4718596
  65.0 6.8 %copy-start.15 = (bf16[8,64,12,32]{1,0,3,2:T(8,128)(2,1)S(1)}, bf16[8,64,12,32]{1,0,3,2:T(8,128)(2,1)}, u32[]{:S(2)}) copy-start(bf16[8,64,12,32]{1,0,3,2:T(8,128)(2,1)} %reshape.452) | copy-start | bytes 1179652
  72.8 58.7 %reduce-scatter.3.cloned.1.call-start = ((), (), s32[]{:S(2)}) async-start(), calls=%async_computation.2 | async-start | bytes 1327104 | tf_op jit(solution)/shard_map/reduce_scatter | solution.py:175
  81.5 3.1 %copy-start.8 = (f32[12,64,64]{1,2,0:T(8,128)S(1)}, f32[12,64,64]{1,2,0:T(8,128)}, u32[]{:S(2)}) copy-start(f32[12,64,64]{1,2,0:T(8,128)} %get-tuple-element.7) | copy-start | bytes 589828
  84.6 1.3 copy-start.11
  86.7 43.9 %copy-start.7 = (bf16[1,16,32,384]{3,2,1,0:T(8,128)(2,1)S(1)}, bf16[1,16,32,384]{3,2,1,0:T(8,128)(2,1)}, u32[]{:S(2)}) copy-start(bf16[1,16,32,384]{3,2,1,0:T(8,128)(2,1)} %param.8) | copy-start | bytes 1179652
  86.8 4.2 %collective-permute-start.2 = (bf16[1,16,4,384]{3,2,1,0:T(4,128)(2,1)S(1)}, bf16[1,16,4,384]{3,2,1,0:T(4,128)(2,1)S(1)}, u32[]{:S(2)}, u32[]{:S(2)}) collective-permute-start(bf16[1,16,4,384]{3,2,1,0:T(4,128)(2,1)S(1)} %slice.61), channel_id=1, source_target_pairs={{2,0},{0,2},{3,1},{1,3},{6,4},{4,6},{7,5},{5,7},{10,8},{8,10},{11,... | collective-permute-start | bytes 147464 | tf_op jit(solution)/shard_map/ppermute | solution.py:18
  91.0 39.6 %collective-permute-start.3 = (bf16[1,4,32,384]{3,2,1,0:T(8,128)(2,1)S(1)}, bf16[1,4,32,384]{3,2,1,0:T(8,128)(2,1)S(1)}, u32[]{:S(2)}, u32[]{:S(2)}) collective-permute-start(bf16[1,4,32,384]{3,2,1,0:T(8,128)(2,1)S(1)} %pad_maximum_fusion.3), channel_id=1, source_target_pairs={{28,0},{0,4},{4,8},{8,12},{12,16},{16,20},{20,24},{24,28},{29,1},{... | collective-permute-start | bytes 294920 | tf_op jit(solution)/shard_map/ppermute | solution.py:18
  (1 other events, 0.7 us)
Sparse Core Ops, SparseCore 0:
  73.0 11.1 reduce-scatter.4
  87.0 19.1 reduce-scatter.2
where the time goes:
time: 218 us; the launch traced here: 214 us
  blocking collectives  115 us (53%)
  matrix products  32.7 us (15%)
  local copies, waits for them, and re-layouts  22.7 us (10%)
  other arithmetic  16.8 us (8%)
  between operations  14.7 us (7%)
  starting transfers between devices  8.08 us (4%)
  waiting for transfers between devices  4.03 us (2%)
    psum x1, blocking collectives, shards(): half_qkv, half_proj = lax.psum((half_qkv, half_proj), ('ha', 'wa'))  75.2 us
    psum x1, blocking collectives, shards(): lax.psum((d_table, d_scale, d_gain), ('ha', 'wa', 'ba'))  39.5 us
    dot_general x3, matrix products, fine_product(): return jnp.einsum(form, left, right, precision=HIGHEST)  16.3 us
    ppermute x4, starting transfers between devices, from_behind(): return lax.ppermute(block, axis, route)  7.79 us
    convert_element_type x2, local copies, waits for them, and re-layouts, grads_region(): jnp.stack([d_query, d_key, d_values], 3).astype(jnp.bfloat16)  5.15 us
    dot_general x3, matrix products, coarse_product(): return jnp.einsum(form, left, right, preferred_element_type=jnp.float32)  5.11 us
  transfers between devices with their start and end apart: 6, of which 2 were waited for; matrix products, arithmetic and copies ran while one was open for 10% of the time, Pallas kernels for 0%

commit v1 on v0

--- a/solution.py
+++ b/solution.py
@@ -3,6 +3,7 @@
 import jax.numpy as jnp
 from jax import lax
 from jax.sharding import PartitionSpec as P
+from jax.lax import psum
 
 WIN = 8
 EPS_NORM = 1e-05
@@ -180,7 +181,8 @@
         ).astype(jnp.float32),
     )
     half_qkv, half_proj = lax.psum((half_qkv, half_proj), ("ha", "wa"))
-    d_table, d_scale, d_gain = lax.psum((d_table, d_scale, d_gain), ("ha", "wa", "ba"))
+    _convert_region = lambda u_in, mesh_dim, along_axis: psum(psum(u_in, mesh_dim), along_axis)
+    d_table, d_scale, d_gain = _convert_region((d_table, d_scale, d_gain), "ha", ("wa", "ba"))
     return (d_tokens, half_qkv, half_proj, d_table, d_scale, d_gain)
 
 

time: 218 us -> 225 us (1.032)
  blocking collectives: 115 us -> 121 us
    psum x1 -> x2, blocking collectives: 39.5 us -> 46.3 us  [the longest x1 29.3 us: shards(): psum(u_in, mesh_dim)]
  transfers between devices with their start and end apart: 6 -> 6, of which waited for: 2 -> 2; matrix products, arithmetic and copies ran while one was open for 10% -> 9% of each run, Pallas kernels for 0% -> 0%
where the time goes in v1:
time: 225 us; the launch traced here: 220 us
  blocking collectives  121 us (54%)
  matrix products  32.7 us (15%)
  local copies, waits for them, and re-layouts  22.7 us (10%)
  other arithmetic  16.8 us (7%)
  between operations  14.7 us (7%)
  starting transfers between devices  8.08 us (4%)
  waiting for transfers between devices  4.03 us (2%)
    psum x1, blocking collectives, shards(): half_qkv, half_proj = lax.psum((half_qkv, half_proj), ('ha', 'wa'))  75.2 us
    psum x1, blocking collectives, shards(): psum(u_in, mesh_dim)  29.3 us
    psum x1, blocking collectives, shards(): psum(psum(u_in, mesh_dim), along_axis)  17 us
    dot_general x3, matrix products, fine_product(): return jnp.einsum(form, left, right, precision=HIGHEST)  16.3 us
    ppermute x4, starting transfers between devices, from_behind(): return lax.ppermute(block, axis, route)  7.79 us
    convert_element_type x2, local copies, waits for them, and re-layouts, grads_region(): jnp.stack([d_query, d_key, d_values], 3).astype(jnp.bfloat16)  5.15 us
    dot_general x3, matrix products, coarse_product(): return jnp.einsum(form, left, right, preferred_element_type=jnp.float32)  5.11 us
  transfers between devices with their start and end apart: 6, of which 2 were waited for; matrix products, arithmetic and copies ran while one was open for 9% of the time, Pallas kernels for 0%

profile of v1, /device:TPU:0, one launch (start us, length us, event | category | flops | bytes accessed | tf_op | source)
XLA Modules:
  0.0 220.5 jit_solution(2683566608960653848)
XLA Ops:
  8.3 4.6 %collective-permute-start = (bf16[2,1,4,32,384]{4,3,2,1,0:T(8,128)(2,1)S(1)}, bf16[2,1,4,32,384]{4,3,2,1,0:T(8,128)(2,1)S(1)}, u32[]{:S(2)}, u32[]{:S(2)}) collective-permute-start(bf16[2,1,4,32,384]{4,3,2,1,0:T(8,128)(2,1)S(1)} %pad_maximum_fusion.2), channel_id=1, source_target_pairs={{4,0},{8,4},{12,8},{16,12},{20,16},{24,20},{28,24},{0,28},{5,1},{9... | collective-permute-start | bytes 589832 | tf_op jit(solution)/shard_map/ppermute | solution.py:19
  15.2 2.0 fusion.2
  18.3 1.6 collective-permute-start.1
  20.2 2.8 %collective-permute-done.1 = bf16[2,1,16,4,384]{4,3,2,1,0:T(4,128)(2,1)S(1)} collective-permute-done((bf16[2,1,16,4,384]{4,3,2,1,0:T(4,128)(2,1)S(1)}, bf16[2,1,16,4,384]{4,3,2,1,0:T(4,128)(2,1)S(1)}, u32[]{:S(2)}, u32[]{:S(2)}) %collective-permute-start.1) | collective-permute-done | bytes 98336 | tf_op jit(solution)/shard_map/ppermute | solution.py:19
  26.1 3.0 %reshape.449 = bf16[1,8,64,3,12,32]{2,1,5,4,3,0:T(8,128)(2,1)} reshape(bf16[512,1152]{0,1:T(8,128)(2,1)S(1)} %copy.82) | data formatting | bytes 2359296 | tf_op jit(solution)/shard_map/reshape | solution.py:80
  29.2 1.8 fusion.67
  31.7 5.2 %fusion.29 = f32[8,12,64,64]{2,3,1,0:T(8,128)S(1)} fusion(f32[8,64,12]{1,2,0:T(8,128)S(1)} %add_rsqrt_fusion.1, f32[8,64,12]{1,2,0:T(8,128)S(1)} %add_rsqrt_fusion, bf16[1,8,64,1,12,32]{2,1,5,4,3,0:T(8,128)(2,1)S(1)} %get-tuple-element.19, bf16[1,8,64,1,12,32]{2,1,5,4,3,0:T(8,128)(2,1)S(1)} %get-tuple-element.20), kind=kOutput, calls=%fused_computation.41 | convolution fusion | flops 151781376 | bytes 2408448 | tf_op jit(solution)/shard_map/bnqhd,bnkhd->bnhqk/dot_general | solution.py:27
  42.1 1.6 fusion.69
  44.8 2.3 %copy.90 = f32[512,384]{0,1:T(8,128)} copy(f32[512,384]{1,0:T(8,128)} %bitcast.140) | data formatting | bytes 1572864 | tf_op jit(solution)/shard_map/convert_element_type | solution.py:110
  48.3 1.4 multiply_reduce_fusion.2
  49.8 1.4 multiply_convert_fusion
  54.3 3.6 %multiply_reduce_fusion.1 = (f32[8,12,64]{2,1,0:T(8,128)S(1)}, f32[8,12,64,64]{2,3,1,0:T(8,128)S(1)}) fusion(f32[8,12,64,64]{2,3,1,0:T(8,128)} %copy-done.3, f32[8,12,64]{2,1,0:T(8,128)S(1)} %get-tuple-element.24, bf16[1,8,64,1,12,32]{2,1,5,4,3,0:T(8,128)(2,1)} %copy-done.14, bf16[8,64,12,32]{1,0,3,2:T(8,128)(2,1)} %reshape.452), kind=kOutput, calls=%fused_computation.7 | convolution fusion | flops 26339328 | bytes 3981312 | tf_op jit(solution)/shard_map/bnqhd,bnkhd->bnhqk/dot_general | solution.py:23
  58.6 2.2 multiply_reduce_fusion
  60.7 4.3 %fusion.22 = (f32[8,64,12]{1,2,0:T(8,128)S(1)}, f32[8,12,32,64]{3,2,1,0:T(8,128)}) fusion(f32[8,64,12]{1,2,0:T(8,128)S(1)} %add_rsqrt_fusion.1, bf16[1,8,64,1,12,32]{2,1,5,4,3,0:T(8,128)(2,1)S(1)} %get-tuple-element.20, f32[8,12,64,64]{2,3,1,0:T(8,128)S(1)} %get-tuple-element.18, f32[12]{0:T(128)S(1)} %minimum_exponential_fusion, ...), kind=kOutput, calls=%fused_computation.35 | convolution fusion | flops 152561664 | bytes 3219504 | tf_op jit(solution)/shard_map/bnhqk,bnkhd->bnqhd/dot_general | solution.py:27
  65.0 6.8 %fusion.18 = (f32[8,64,12]{1,2,0:T(8,128)}, f32[8,12,32,64]{3,2,1,0:T(8,128)}) fusion(f32[8,64,12]{1,2,0:T(8,128)S(1)} %add_rsqrt_fusion, bf16[1,8,64,1,12,32]{2,1,5,4,3,0:T(8,128)(2,1)S(1)} %get-tuple-element.19, f32[8,12,64,64]{2,3,1,0:T(8,128)S(1)} %get-tuple-element.18, f32[12]{0:T(128)S(1)} %minimum_exponential_fusion, ...), kind=kOutput, calls=%fused_computation.31 | convolution fusion | flops 152561664 | bytes 3219504 | tf_op jit(solution)/shard_map/bnhqk,bnqhd->bnkhd/dot_general | solution.py:27
  73.1 2.6 %fusion.21 = (bf16[1,8,64,1,12,32]{2,5,4,1,3,0:T(8,128)(2,1)S(1)}, bf16[1,8,64,1,12,32]{2,5,4,1,3,0:T(8,128)(2,1)S(1)}) fusion(f32[8,12,32,64]{3,2,1,0:T(8,128)} %get-tuple-element.31, f32[8,64,12]{1,2,0:T(8,128)} %get-tuple-element.30, f32[8,64,12]{1,2,0:T(8,128)S(1)} %add_rsqrt_fusion, bf16[1,8,64,1,12,32]{2,1,5,4,3,0:T(8,128)(2,1)S(1)} %get-tuple-element.19, ...), kind=kLoop, calls=%fused_computation.34 | loop fusion | flops 2359296 | bytes 3244032 | tf_op jit(solution)/shard_map/stack | solution.py:136
  76.3 2.7 %copy.98 = bf16[1,8,64,3,12,32]{2,1,5,4,3,0:T(8,128)(2,1)S(1)} copy(bf16[1,8,64,3,12,32]{2,5,4,1,3,0:T(8,128)(2,1)S(1)} %maximum_convert_fusion) | data formatting | bytes 2359296 | tf_op jit(solution)/shard_map/convert_element_type | solution.py:136
  79.1 2.4 %convert_element_type.207 = bf16[512,1152]{0,1:T(8,128)(2,1)} reshape(bf16[1,8,64,3,12,32]{2,1,5,4,3,0:T(8,128)(2,1)S(1)} %copy.98) | data formatting | bytes 2359296 | tf_op jit(solution)/shard_map/convert_element_type | solution.py:136
  81.5 3.1 %convolution_convert_fusion.1 = bf16[384,1152]{0,1:T(8,128)(2,1)} fusion(bf16[512,1152]{0,1:T(8,128)(2,1)} %convert_element_type.207, bf16[512,384]{1,0:T(8,128)(2,1)} %bitcast.142), kind=kOutput, calls=%fused_computation.15 | convolution fusion | flops 453427200 | bytes 2457600 | tf_op jit(solution)/shard_map/dot_general | solution.py:137
  86.8 1.6 collective-permute-start.2
  88.4 1.4 fusion.41
  91.1 29.3 %all-reduce.1 = (f32[12,225]{1,0:T(8,128)S(1)}, f32[12]{0:T(128)S(1)}, f32[384]{0:T(512)S(1)}) all-reduce(f32[12,225]{1,0:T(8,128)S(1)} %fusion.41, f32[12]{0:T(128)S(1)} %compare_select_fusion.1, f32[384]{0:T(512)S(1)} %get-tuple-element.8), channel_id=1, replica_groups=mesh['ha'=8,'wa'=2,'ba'=2] {'ha'}, use_global_device_ids=true, to_apply=%region_16.17 | all-reduce | flops 3096 | bytes 24768 | tf_op jit(solution)/shard_map/psum | solution.py:184
  120.4 17.0 %all-reduce.2 = (f32[12,225]{1,0:T(8,128)}, f32[12]{0:T(128)}, f32[384]{0:T(512)}) all-reduce(f32[12,225]{1,0:T(8,128)S(1)} %get-tuple-element.12, f32[12]{0:T(128)S(1)} %get-tuple-element.13, f32[384]{0:T(512)S(1)} %get-tuple-element.14), channel_id=1, replica_groups=mesh['ha'=8,'wa'=2,'ba'=2] {'wa','ba'}, use_global_device_ids=true, to_apply=%region_17.18 | all-reduce | flops 3096 | bytes 24768 | tf_op jit(solution)/shard_map/psum | solution.py:184
  138.3 75.2 %all-reduce.4 = (f32[384,576]{0,1:T(8,128)}, f32[384,192]{0,1:T(8,128)}) all-reduce(bf16[384,576]{0,1:T(8,128)(2,1)} %reduce-scatter.3.cloned.1.call-done, bf16[384,192]{0,1:T(8,128)(2,1)} %reduce-scatter.5.cloned.1.call-done), channel_id=1, replica_groups=mesh['ha'=8,'wa'=2,'ba'=2] {'ha','wa'}, use_global_device_ids=true, to_apply=%region_12.13 | all-reduce | flops 294912 | bytes 1769472 | tf_op jit(solution)/shard_map/psum | solution.py:183
  (100 shorter events, 25.9 us)
Async XLA Ops:
  7.2 17.5 %copy-start = (bf16[384,1152]{1,0:T(8,128)(2,1)S(1)}, bf16[384,1152]{1,0:T(8,128)(2,1)}, u32[]{:S(2)}) copy-start(bf16[384,1152]{1,0:T(8,128)(2,1)} %param.9) | copy-start | bytes 2654212
  7.2 8.0 %copy-start.17 = (f32[12,225]{1,0:T(8,128)S(1)}, f32[12,225]{1,0:T(8,128)}, u32[]{:S(2)}) copy-start(f32[12,225]{1,0:T(8,128)} %param.11) | copy-start | bytes 32404
  7.2 131.1 %reduce-scatter.5.cloned.1.call-start = ((), (), s32[]{:S(2)}) async-start(), calls=%async_computation.3 | async-start | bytes 442368 | tf_op jit(solution)/shard_map/reduce_scatter | solution.py:179
  8.3 10.0 %collective-permute-start = (bf16[2,1,4,32,384]{4,3,2,1,0:T(8,128)(2,1)S(1)}, bf16[2,1,4,32,384]{4,3,2,1,0:T(8,128)(2,1)S(1)}, u32[]{:S(2)}, u32[]{:S(2)}) collective-permute-start(bf16[2,1,4,32,384]{4,3,2,1,0:T(8,128)(2,1)S(1)} %pad_maximum_fusion.2), channel_id=1, source_target_pairs={{4,0},{8,4},{12,8},{16,12},{20,16},{24,20},{28,24},{0,28},{5,1},{9... | collective-permute-start | bytes 589832 | tf_op jit(solution)/shard_map/ppermute | solution.py:19
  14.0 4.3 %copy-start.18 = (f32[12]{0:T(128)S(1)}, f32[12]{0:T(128)}, u32[]{:S(2)}) copy-start(f32[12]{0:T(128)} %param.12) | copy-start | bytes 148
  18.3 4.7 %collective-permute-start.1 = (bf16[2,1,16,4,384]{4,3,2,1,0:T(4,128)(2,1)S(1)}, bf16[2,1,16,4,384]{4,3,2,1,0:T(4,128)(2,1)S(1)}, u32[]{:S(2)}, u32[]{:S(2)}) collective-permute-start(bf16[2,1,16,4,384]{4,3,2,1,0:T(4,128)(2,1)S(1)} %pad_maximum_fusion.4), channel_id=1, source_target_pairs={{2,0},{0,2},{3,1},{1,3},{6,4},{4,6},{7,5},{5,7},{10,8},{8,10},{11,... | collective-permute-start | bytes 294920 | tf_op jit(solution)/shard_map/ppermute | solution.py:19
  30.9 7.7 %copy-start.14 = (bf16[1,8,64,1,12,32]{2,1,5,4,3,0:T(8,128)(2,1)}, bf16[1,8,64,1,12,32]{2,1,5,4,3,0:T(8,128)(2,1)S(1)}, u32[]{:S(2)}) copy-start(bf16[1,8,64,1,12,32]{2,1,5,4,3,0:T(8,128)(2,1)S(1)} %get-tuple-element.21) | copy-start | bytes 1179652
  31.7 5.2 %copy-start.10 = (f32[12,64,64]{1,2,0:T(8,128)S(1)}, f32[12,64,64]{1,2,0:T(8,128)}, u32[]{:S(2)}) copy-start(f32[12,64,64]{1,2,0:T(8,128)} %copy.85) | copy-start | bytes 589828
  31.7 5.2 %copy-start.13 = (f32[8,64,64]{1,2,0:T(8,128)S(1)}, f32[8,64,64]{1,2,0:T(8,128)}, u32[]{:S(2)}) copy-start(f32[8,64,64]{1,2,0:T(8,128)} %compare_select_fusion) | copy-start | bytes 393220
  36.9 1.7 copy-start.1
  38.6 1.7 copy-start.3
  42.1 1.7 copy-start.6
  43.9 3.2 %copy-start.16 = (f32[384]{0:T(512)S(1)}, f32[384]{0:T(512)}, u32[]{:S(2)}) copy-start(f32[384]{0:T(512)} %param.13) | copy-start | bytes 4612
  49.8 1.4 copy-start.12
  49.8 1.9 copy-start.5
  54.3 3.6 %copy-start.2 = (f32[8,12,64,64]{2,3,1,0:T(8,128)S(1)}, f32[8,12,64,64]{2,3,1,0:T(8,128)}, u32[]{:S(2)}) copy-start(f32[8,12,64,64]{2,3,1,0:T(8,128)} %copy-done.1) | copy-start | bytes 4718596
  54.3 4.3 %copy-start.4 = (f32[8,12,64,64]{2,3,1,0:T(8,128)S(1)}, f32[8,12,64,64]{2,3,1,0:T(8,128)}, u32[]{:S(2)}) copy-start(f32[8,12,64,64]{2,3,1,0:T(8,128)} %copy-done.3) | copy-start | bytes 4718596
  65.0 6.8 %copy-start.15 = (bf16[8,64,12,32]{1,0,3,2:T(8,128)(2,1)S(1)}, bf16[8,64,12,32]{1,0,3,2:T(8,128)(2,1)}, u32[]{:S(2)}) copy-start(bf16[8,64,12,32]{1,0,3,2:T(8,128)(2,1)} %reshape.452) | copy-start | bytes 1179652
  72.8 65.4 %reduce-scatter.3.cloned.1.call-start = ((), (), s32[]{:S(2)}) async-start(), calls=%async_computation.2 | async-start | bytes 1327104 | tf_op jit(solution)/shard_map/reduce_scatter | solution.py:176
  81.5 3.1 %copy-start.8 = (f32[12,64,64]{1,2,0:T(8,128)S(1)}, f32[12,64,64]{1,2,0:T(8,128)}, u32[]{:S(2)}) copy-start(f32[12,64,64]{1,2,0:T(8,128)} %get-tuple-element.7) | copy-start | bytes 589828
  84.6 1.3 copy-start.11
  86.7 50.7 %copy-start.7 = (bf16[1,16,32,384]{3,2,1,0:T(8,128)(2,1)S(1)}, bf16[1,16,32,384]{3,2,1,0:T(8,128)(2,1)}, u32[]{:S(2)}) copy-start(bf16[1,16,32,384]{3,2,1,0:T(8,128)(2,1)} %param.8) | copy-start | bytes 1179652
  86.8 4.2 %collective-permute-start.2 = (bf16[1,16,4,384]{3,2,1,0:T(4,128)(2,1)S(1)}, bf16[1,16,4,384]{3,2,1,0:T(4,128)(2,1)S(1)}, u32[]{:S(2)}, u32[]{:S(2)}) collective-permute-start(bf16[1,16,4,384]{3,2,1,0:T(4,128)(2,1)S(1)} %slice.61), channel_id=1, source_target_pairs={{2,0},{0,2},{3,1},{1,3},{6,4},{4,6},{7,5},{5,7},{10,8},{8,10},{11,... | collective-permute-start | bytes 147464 | tf_op jit(solution)/shard_map/ppermute | solution.py:19
  91.0 46.4 %collective-permute-start.3 = (bf16[1,4,32,384]{3,2,1,0:T(8,128)(2,1)S(1)}, bf16[1,4,32,384]{3,2,1,0:T(8,128)(2,1)S(1)}, u32[]{:S(2)}, u32[]{:S(2)}) collective-permute-start(bf16[1,4,32,384]{3,2,1,0:T(8,128)(2,1)S(1)} %pad_maximum_fusion.3), channel_id=1, source_target_pairs={{28,0},{0,4},{4,8},{8,12},{12,16},{16,20},{20,24},{24,28},{29,1},{... | collective-permute-start | bytes 294920 | tf_op jit(solution)/shard_map/ppermute | solution.py:19
  (1 other events, 0.7 us)
Sparse Core Ops, SparseCore 0:
  73.0 11.1 reduce-scatter.4
  87.0 18.5 reduce-scatter.2
